TPU v7x, 32 devices: a whole 2x2x4 slice. The times are simulated.
32 devices in a mesh: fact: 8 (over z, x), dim: 4 (over y, core).
Axes of the slice: x: 2, y: 2, z: 4, core: 2. Of those that a mesh axis runs over, the one named last changes fastest.
Arguments:
- fact_keys: int32 [1048576], P(('fact', 'dim')), may hold values from 0 to 65535, as said below
- revenue: bfloat16 [1048576], P(('fact', 'dim')), may hold values from 0.099609375 to 1
- filter_bits: int32 [256, 256], replicated, may hold values from 0 to 1
- categories: int32 [65536], P(('fact', 'dim')), may hold values from 0 to 511
- attributes: bfloat16 [65536, 128], P(('fact', 'dim')), may hold values from -0.125 to 0.125
Outputs:
- category_totals: float32 [512, 128], P(('fact', 'dim'))
Inputs may be any that keep to these rules, and one draw needn't show every extreme that they name: `fact_keys`: keys of owner o are o * 2048 to (o + 1) * 2048 - 1. Among the 32768 rows of one device at most 2048 have keys of any one owner; in every draw one owner gets exactly 2048 matching rows from every device, and every device has exactly 2048 matching rows for some owner.
All inputs are finite; a program needn't handle non-finite values.
Results may differ from a plain program's by a relative error of at most 0.0003.
Values may be sent and summed in bfloat16 or wider, within the bound.
A program may use at most 64 MiB of HBM per device.

v0:
```python
import math

import jax
import jax.numpy as jnp
from jax import lax
from jax.sharding import PartitionSpec as P

CATS = 512


def category_sums(own_sums, categories, attributes):
    weighted = own_sums[:, None] * attributes.astype(jnp.float32)
    cat_hot = (categories[:, None] == jnp.arange(CATS, dtype=jnp.int32)[None, :]).astype(
        jnp.float32
    )
    return lax.dot_general(
        cat_hot,
        weighted,
        (((0,), (0,)), ((), ())),
        precision=lax.Precision.HIGHEST,
        preferred_element_type=jnp.float32,
    )


def per_device(fact_keys, revenue, filter_bits, categories, attributes):
    rows = fact_keys.shape[0]
    key_hi, key_lo = filter_bits.shape
    filt = filter_bits.astype(jnp.bfloat16)
    block = math.gcd(rows, 2048)
    keys_blocks = fact_keys.reshape(rows // block, block)
    rev_blocks = revenue.reshape(rows // block, block)
    high_ids = jnp.arange(key_hi, dtype=jnp.int32)
    low_ids = jnp.arange(key_lo, dtype=jnp.int32)
    zero_half = jnp.zeros((), jnp.bfloat16)

    def probe_block(item):
        keys, rev = item
        high = (keys[:, None] // key_lo == high_ids[None, :]).astype(jnp.bfloat16)
        low = keys[:, None] % key_lo == low_ids[None, :]
        passing = jnp.dot(high, filt, preferred_element_type=jnp.float32)
        match = jnp.sum(jnp.where(low, passing, 0.0), axis=1)
        return (high, low, match)

    def add_sums(carry, item):
        high, low, match = probe_block(item)
        scaled = item[1] * match.astype(jnp.bfloat16)
        weighted_low = jnp.where(low, scaled[:, None], zero_half)
        term = lax.dot_general(
            high, weighted_low, (((0,), (0,)), ((), ())), preferred_element_type=jnp.float32
        )
        return (carry + term, None)

    totals, _ = lax.scan(
        add_sums, jnp.zeros((key_hi, key_lo), jnp.float32), (keys_blocks, rev_blocks)
    )
    own_sums = lax.psum_scatter(
        totals.reshape(-1), ("fact", "dim"), scatter_dimension=0, tiled=True
    )
    partial_totals = category_sums(own_sums, categories, attributes)
    return lax.psum_scatter(partial_totals, ("fact", "dim"), scatter_dimension=0, tiled=True)


def solution(mesh):
    in_specs = (
        P(("fact", "dim")),
        P(("fact", "dim")),
        P(),
        P(("fact", "dim")),
        P(("fact", "dim"), None),
    )
    out_specs = P(("fact", "dim"), None)
    return jax.shard_map(
        per_device, mesh=mesh, in_specs=in_specs, out_specs=out_specs, check_vma=False
    )
```

profile of v0, /device:TPU:0, one launch (start us, length us, event | category | flops | bytes accessed | tf_op | source)
XLA Modules:
  0.0 311.7 jit_solution(16808163438264407972)
XLA Ops:
  6.5 0.0 copy-start
  6.5 0.0 all-reduce.3.cloned.1.call-start
  6.5 1.0 convert_element_type.20
  7.5 0.9 reshape.119
  8.5 0.0 copy-done
  8.5 25.7 %while.15 = (s32[]{:T(128)}, f32[256,256]{1,0:T(8,128)S(1)}, s32[16,2048]{1,0:T(8,128)S(1)}, bf16[16,2048]{1,0:T(8,128)(2,1)S(1)}, bf16[256,256]{1,0:T(8,128)(2,1)S(1)}, /*index=5*/s32[]{:T(128)}, s32[]{:T(128)}) while((s32[]{:T(128)}, f32[256,256]{1,0:T(8,128)S(1)}, s32[16,2048]{1,0:T(8,128)S(1)}, ...), condition=%wide.region_2.3_spmd.clone.clone, body=%wide.region_0.2_spmd.clone.clone.sunk | while | flops 540710912 | bytes 757855 | solution.py:53
  8.6 0.7 fusion.27
  9.4 0.7 fusion.28
  10.2 0.7 fusion.27
  11.0 0.7 fusion.28
  11.8 0.7 fusion.27
  12.6 0.7 fusion.28
  13.4 0.7 fusion.27
  14.2 0.7 fusion.28
  15.0 0.7 fusion.27
  15.8 0.7 fusion.28
  16.6 0.7 fusion.27
  17.4 0.7 fusion.28
  18.2 0.7 fusion.27
  19.0 0.7 fusion.28
  19.8 0.7 fusion.27
  20.6 0.7 fusion.28
  21.4 0.7 fusion.27
  22.2 0.7 fusion.28
  23.0 0.7 fusion.27
  23.8 0.7 fusion.28
  24.6 0.7 fusion.27
  25.4 0.7 fusion.28
  26.2 0.7 fusion.27
  27.0 0.7 fusion.28
  27.8 0.7 fusion.27
  28.6 0.7 fusion.28
  29.4 0.7 fusion.27
  30.2 0.7 fusion.28
  31.0 0.7 fusion.27
  31.8 0.7 fusion.28
  32.6 0.7 fusion.27
  33.4 0.7 fusion.28
  34.2 0.0 copy-start.1
  34.2 0.0 copy-start.2
  34.2 0.8 copy.8
  35.1 0.0 all-reduce.3.cloned.1.call-update
  35.1 0.0 reduce-scatter.2.cloned.1.call-start
  35.1 129.4 %all-reduce.3.cloned.1.call-done = f32[65536]{0:T(1024)} async-done(((f32[65536]{0:T(1024)}), f32[65536]{0:T(1024)}) %all-reduce.3.cloned.1.call-update) | async-done | bytes 262160
  164.6 0.7 dynamic-slice
  165.3 0.0 copy-done.1
  165.3 0.0 copy-done.2
  165.3 4.7 %fusion.15 = f32[512,128]{1,0:T(8,128)} fusion(s32[2048]{0:T(1024)S(1)} %copy-done.2, bf16[2048,128]{1,0:T(8,128)(2,1)S(1)} %copy-done.1, f32[2048]{0:T(1024)S(1)} %dynamic-slice), kind=kOutput, calls=%fused_computation.26 | convolution fusion | flops 1612185600 | bytes 802816 | tf_op jit(solution)/shard_map/dot_general | solution.py:16
  170.0 0.0 reduce-scatter.2.cloned.1.call-update
  170.0 134.8 %reduce-scatter.2.cloned.1.call-done = f32[16,128]{1,0:T(8,128)} async-done(((f32[512,128]{1,0:T(8,128)}), f32[16,128]{1,0:T(8,128)}) %reduce-scatter.2.cloned.1.call-update) | async-done | bytes 8208 | tf_op jit(solution)/shard_map/reduce_scatter | solution.py:60
  (66 shorter events, 1.3 us)
Async XLA Ops:
  6.5 1.9 copy-start
  6.5 158.0 %all-reduce.3.cloned.1.call-start = ((), (), s32[]{:S(2)}) async-start(), calls=%async_computation.2 | async-start | bytes 524288
  34.2 131.1 %copy-start.1 = (bf16[2048,128]{1,0:T(8,128)(2,1)S(1)}, bf16[2048,128]{1,0:T(8,128)(2,1)}, u32[]{:S(2)}) copy-start(bf16[2048,128]{1,0:T(8,128)(2,1)} %param.11) | copy-start | bytes 1572868
  34.2 131.1 %copy-start.2 = (s32[2048]{0:T(1024)S(1)}, s32[2048]{0:T(1024)}, u32[]{:S(2)}) copy-start(s32[2048]{0:T(1024)} %param.10) | copy-start | bytes 24580
  35.1 269.7 %reduce-scatter.2.cloned.1.call-start = ((), (), s32[]{:S(2)}) async-start(), calls=%async_computation.1 | async-start | bytes 270336 | tf_op jit(solution)/shard_map/reduce_scatter | solution.py:60
Sparse Core Ops, SparseCore 0:
  35.2 129.3 all-reduce.2
  170.1 134.6 reduce-scatter.1
where the time goes:
time: 312 us
  waiting for transfers between devices  264 us (85%)
  matrix products  28.3 us (9%)
  between operations  13.5 us (4%)
  local copies, waits for them, and re-layouts  3.44 us (1%)
    reduce_scatter x1, waiting for transfers between devices, per_device(): lax.psum_scatter(partial_totals, ('fact', 'dim'), scatter_dimension=0, ti...  135 us
    unnamed x3, waiting for transfers between devices  129 us
    dot_general x16, matrix products, add_sums(): lax.dot_general(high, weighted_low, (((0,), (0,)), ((), ())), preferred_e...  12 us
    dot_general x16, matrix products, probe_block(): passing = jnp.dot(high, filt, preferred_element_type=jnp.float32)  11.6 us
  transfers between devices with their start and end apart: 2, of which 2 were waited for; matrix products, arithmetic and copies ran while one was open for 0% of the time, Pallas kernels for 0%

commit v1 on v0

v1 whole, which is shorter than its diff:
```python
import functools

import jax
import jax.numpy as jnp
from jax import lax
from jax.experimental import pallas as pl
from jax.experimental.pallas import tpu as pltpu
from jax.sharding import PartitionSpec as P

CATS = 512
LANES = 128
MESH = pl.DeviceIdType.MESH


def rows_of(row, count):
    packed = jnp.broadcast_to(row, (16, LANES)).astype(jnp.bfloat16)
    return jnp.concatenate([packed] * (count // 16), axis=0)


def ids_of(count):
    return lax.broadcasted_iota(jnp.int32, (count, LANES), 0).astype(jnp.float32).astype(jnp.bfloat16)


def kernel(
    n_fact,
    n_dim,
    keys_ref,
    rev_ref,
    filt_ref,
    cat_ref,
    attr_ref,
    out_ref,
    high_ref,
    low_ref,
    value_ref,
    acc_ref,
    send1,
    recv1,
    weight_ref,
    send2,
    recv2,
    send_sem1,
    recv_sem1,
    send_sem2,
    recv_sem2,
):
    n = n_fact * n_dim
    me = lax.axis_index("fact") * n_dim + lax.axis_index("dim")
    key_hi, key_lo = acc_ref.shape
    own_rows = key_hi // n
    cat_rows = CATS // n

    def device(peer):
        return (peer // n_dim, lax.rem(peer, n_dim))

    def peer_at(step):
        return lax.rem(me + step, n)

    barrier = pltpu.get_barrier_semaphore()

    def greet(step, carry):
        pl.semaphore_signal(barrier, inc=1, device_id=device(peer_at(step)), device_id_type=MESH)
        return carry

    lax.fori_loop(1, n, greet, 0)

    keys = keys_ref[...]
    high_ref[...] = (keys // key_lo).astype(jnp.float32)
    low_ref[...] = lax.rem(keys, key_lo).astype(jnp.float32)
    value_ref[...] = rev_ref[...].astype(jnp.float32)
    acc_ref[...] = jnp.zeros_like(acc_ref)

    lines = keys_ref.shape[0]
    step_lines = 8
    one = jnp.ones((), jnp.bfloat16)
    zero = jnp.zeros((), jnp.bfloat16)

    def add_block(block, carry):
        high_ids = ids_of(key_hi)
        low_ids = ids_of(key_lo)
        hots, weighted = [], []
        for j in range(step_lines):
            line = pl.ds(block * step_lines + j, 1)
            high = rows_of(high_ref[line, :], key_hi)
            low = rows_of(low_ref[line, :], key_lo)
            value = rows_of(value_ref[line, :], key_lo)
            hots.append(jnp.where(high == high_ids, one, zero))
            weighted.append(jnp.where(low == low_ids, value, zero))
        acc_ref[...] += lax.dot_general(
            jnp.concatenate(hots, axis=1),
            jnp.concatenate(weighted, axis=1),
            (((1,), (1,)), ((), ())),
            preferred_element_type=jnp.float32,
        )
        return carry

    lax.fori_loop(0, lines // step_lines, add_block, 0)

    for o in range(n):
        send1[o] = acc_ref[o * own_rows : (o + 1) * own_rows, :]

    pl.semaphore_wait(barrier, n - 1)

    def exchange(send, recv, send_sem, recv_sem):
        def copy_to(peer):
            return pltpu.make_async_remote_copy(
                src_ref=send.at[peer],
                dst_ref=recv.at[me],
                send_sem=send_sem.at[peer],
                recv_sem=recv_sem.at[me],
                device_id=device(peer),
                device_id_type=MESH,
            )

        def start(step, carry):
            copy_to(peer_at(step)).start()
            return carry

        lax.fori_loop(1, n, start, 0)

        def receive(step, total):
            peer = lax.rem(me + n - step, n)
            pltpu.make_async_remote_copy(
                src_ref=send.at[peer],
                dst_ref=recv.at[peer],
                send_sem=send_sem.at[peer],
                recv_sem=recv_sem.at[peer],
                device_id=device(peer),
                device_id_type=MESH,
            ).wait_recv()
            return total + recv[peer]

        total = lax.fori_loop(1, n, receive, send[me])

        def finish():
            def wait(step, carry):
                copy_to(peer_at(step)).wait_send()
                return carry

            lax.fori_loop(1, n, wait, 0)

        return total, finish

    sums, finish1 = exchange(send1, recv1, send_sem1, recv_sem1)
    sums = jnp.where(filt_ref[me] == 1, sums, 0.0)

    half = CATS // 2
    ids = ids_of(half)
    per_row = key_lo // LANES
    for j in range(own_rows * per_row):
        r, c = j // per_row, j % per_row
        own = sums[r : r + 1, c * LANES : (c + 1) * LANES]
        cat = cat_ref[j : j + 1, :]
        upper = cat >= half
        match = rows_of(jnp.where(upper, cat - half, cat).astype(jnp.float32), half) == ids
        first = own.astype(jnp.bfloat16).astype(jnp.float32)
        for t, term in enumerate((first, own - first)):
            for h in range(2):
                part = jnp.where(upper == (h == 1), term, 0.0)
                base = t * CATS + h * half
                weight_ref[base : base + half, j * LANES : (j + 1) * LANES] = jnp.where(
                    match, rows_of(part, half), zero
                )
    attrs = attr_ref[...]
    totals = jnp.dot(
        weight_ref[:CATS, :], attrs, preferred_element_type=jnp.float32
    ) + jnp.dot(weight_ref[CATS:, :], attrs, preferred_element_type=jnp.float32)
    for o in range(n):
        send2[o] = totals[o * cat_rows : (o + 1) * cat_rows, :]
    result, finish2 = exchange(send2, recv2, send_sem2, recv_sem2)
    out_ref[...] = result
    finish1()
    finish2()


def solution(mesh):
    n_fact, n_dim = mesh.shape["fact"], mesh.shape["dim"]
    n = n_fact * n_dim

    def per_device(fact_keys, revenue, filter_bits, categories, attributes):
        rows = fact_keys.shape[0]
        key_hi, key_lo = filter_bits.shape
        own, width = attributes.shape
        lines = rows // LANES
        sums_shape = (n, key_hi // n, key_lo)
        part_shape = (n, CATS // n, width)
        vmem = pl.BlockSpec(memory_space=pltpu.VMEM)
        return pl.pallas_call(
            functools.partial(kernel, n_fact, n_dim),
            out_shape=jax.ShapeDtypeStruct((CATS // n, width), jnp.float32),
            in_specs=[vmem] * 5,
            out_specs=vmem,
            scratch_shapes=[
                pltpu.VMEM((lines, LANES), jnp.float32),
                pltpu.VMEM((lines, LANES), jnp.float32),
                pltpu.VMEM((lines, LANES), jnp.float32),
                pltpu.VMEM((key_hi, key_lo), jnp.float32),
                pltpu.VMEM(sums_shape, jnp.float32),
                pltpu.VMEM(sums_shape, jnp.float32),
                pltpu.VMEM((2 * CATS, own), jnp.bfloat16),
                pltpu.VMEM(part_shape, jnp.float32),
                pltpu.VMEM(part_shape, jnp.float32),
                pltpu.SemaphoreType.DMA((n,)),
                pltpu.SemaphoreType.DMA((n,)),
                pltpu.SemaphoreType.DMA((n,)),
                pltpu.SemaphoreType.DMA((n,)),
            ],
            compiler_params=pltpu.CompilerParams(collective_id=0, has_side_effects=True),
        )(
            fact_keys.reshape(lines, LANES),
            revenue.reshape(lines, LANES),
            filter_bits.reshape(n, key_hi // n, key_lo),
            categories.reshape(own // LANES, LANES),
            attributes,
        )

    split = P(("fact", "dim"))
    return jax.shard_map(
        per_device,
        mesh=mesh,
        in_specs=(split, split, P(), split, P(("fact", "dim"), None)),
        out_specs=P(("fact", "dim"), None),
        check_vma=False,
    )
```

time: 312 us -> 34.7 us (0.11)
  the two profiles are of different devices: /device:TPU:0 before, /device:TPU:25 now
where the time goes in v1:
time: 34.7 us; the launch traced here: 34.5 us
  Pallas kernels  33.2 us (96%)
  local copies, waits for them, and re-layouts  1.3 us (4%)
    pallas_call x1, Pallas kernels, per_device(): pl.pallas_call(functools.partial(kernel, n_fact, n_dim), out_shape=jax.Sh...  33.2 us
    unnamed x1, local copies, waits for them, and re-layouts  1.3 us

profile of v1, /device:TPU:25, one launch (start us, length us, event | category | flops | bytes accessed | tf_op | source)
XLA Modules:
  0.0 34.5 jit_solution(17576896530914632438)
XLA Ops:
  0.0 33.2 %shard_map.55 = f32[16,128]{1,0:T(8,128)} custom-call(s32[256,128]{1,0:T(8,128)} %bitcast.5, bf16[256,128]{1,0:T(8,128)(2,1)} %bitcast.6, s32[32,8,256]{2,1,0:T(8,128)} %bitcast.4, s32[16,128]{1,0:T(8,128)} %bitcast.7, bf16[2048,128]{1,0:T(8,128)(2,1)} %attr_ref.1), custom_call_target="tpu_custom_call" | custom-call | tf_op jit(solution)/shard_map/pallas_call | solution.py:188
  33.2 1.3 %copy.7 = f32[16,128]{1,0:T(8,128)} copy(f32[16,128]{1,0:T(8,128)} %shard_map.55) | data formatting | bytes 16384

commit v2 on v1

--- a/solution.py
+++ b/solution.py
@@ -26,26 +26,38 @@
     n_dim,
     keys_ref,
     rev_ref,
-    filt_ref,
-    cat_ref,
-    attr_ref,
+    filt_hbm,
+    cat_hbm,
+    attr_hbm,
     out_ref,
     high_ref,
     low_ref,
     value_ref,
     acc_ref,
+    filt_ref,
+    cat_ref,
+    attr_ref,
+    weight_ref,
+    local1,
+    pair1,
     send1,
     recv1,
-    weight_ref,
+    local2,
+    pair2,
     send2,
     recv2,
+    load_sem,
+    pair_sem,
     send_sem1,
     recv_sem1,
     send_sem2,
     recv_sem2,
 ):
     n = n_fact * n_dim
+    chips = n // 2
     me = lax.axis_index("fact") * n_dim + lax.axis_index("dim")
+    core, chip = lax.rem(me, 2), me // 2
+    partner = me + 1 - 2 * core
     key_hi, key_lo = acc_ref.shape
     own_rows = key_hi // n
     cat_rows = CATS // n
@@ -53,16 +65,35 @@
     def device(peer):
         return (peer // n_dim, lax.rem(peer, n_dim))
 
-    def peer_at(step):
-        return lax.rem(me + step, n)
+    bits = [1 << b for b in range(chips.bit_length() - 1)]
+    flips = chips == 1 << len(bits)
+
+    def chip_at(step):
+        if not flips:
+            return lax.rem(chip + step, chips)
+        peer = 0
+        for bit in bits:
+            digit = lax.rem(chip // bit, 2)
+            peer += (1 - digit if step & bit else digit) * bit
+        return peer
+
+    def source_at(step):
+        return chip_at(step) if flips else lax.rem(chip + chips - step, chips)
+
+    targets = [chip_at(step) for step in range(1, chips)][::-1]
+    sources = [source_at(step) for step in range(1, chips)]
+
+    loads = [
+        pltpu.make_async_copy(attr_hbm, attr_ref, load_sem.at[0]),
+        pltpu.make_async_copy(filt_hbm.at[me], filt_ref, load_sem.at[1]),
+        pltpu.make_async_copy(cat_hbm, cat_ref, load_sem.at[2]),
+    ]
+    for load in loads:
+        load.start()
 
     barrier = pltpu.get_barrier_semaphore()
-
-    def greet(step, carry):
-        pl.semaphore_signal(barrier, inc=1, device_id=device(peer_at(step)), device_id_type=MESH)
-        return carry
-
-    lax.fori_loop(1, n, greet, 0)
+    for peer in [partner] + [t * 2 + core for t in targets]:
+        pl.semaphore_signal(barrier, inc=1, device_id=device(peer), device_id_type=MESH)
 
     keys = keys_ref[...]
     high_ref[...] = (keys // key_lo).astype(jnp.float32)
@@ -97,52 +128,61 @@
     lax.fori_loop(0, lines // step_lines, add_block, 0)
 
     for o in range(n):
-        send1[o] = acc_ref[o * own_rows : (o + 1) * own_rows, :]
-
-    pl.semaphore_wait(barrier, n - 1)
-
-    def exchange(send, recv, send_sem, recv_sem):
-        def copy_to(peer):
-            return pltpu.make_async_remote_copy(
+        local1[o % 2, o // 2] = acc_ref[o * own_rows : (o + 1) * own_rows, :]
+
+    pl.semaphore_wait(barrier, chips)
+
+    def exchange(local, pair, send, recv, sems, send_sem, recv_sem):
+        swap = pltpu.make_async_remote_copy(
+            src_ref=local.at[1 - core],
+            dst_ref=pair,
+            send_sem=pair_sem.at[sems],
+            recv_sem=pair_sem.at[sems + 1],
+            device_id=device(partner),
+            device_id_type=MESH,
+        )
+        swap.start()
+        swap.wait_recv()
+        send[...] = local[core] + pair[...]
+        copies = [
+            pltpu.make_async_remote_copy(
                 src_ref=send.at[peer],
-                dst_ref=recv.at[me],
+                dst_ref=recv.at[chip],
                 send_sem=send_sem.at[peer],
-                recv_sem=recv_sem.at[me],
-                device_id=device(peer),
+                recv_sem=recv_sem.at[chip],
+                device_id=device(peer * 2 + core),
                 device_id_type=MESH,
             )
-
-        def start(step, carry):
-            copy_to(peer_at(step)).start()
-            return carry
-
-        lax.fori_loop(1, n, start, 0)
-
-        def receive(step, total):
-            peer = lax.rem(me + n - step, n)
-            pltpu.make_async_remote_copy(
-                src_ref=send.at[peer],
-                dst_ref=recv.at[peer],
-                send_sem=send_sem.at[peer],
-                recv_sem=recv_sem.at[peer],
-                device_id=device(peer),
-                device_id_type=MESH,
-            ).wait_recv()
-            return total + recv[peer]
-
-        total = lax.fori_loop(1, n, receive, send[me])
+            for peer in targets
+        ]
+        for copy in copies:
+            copy.start()
+
+        def receive():
+            total = send[chip]
+            for peer in sources:
+                pltpu.make_async_remote_copy(
+                    src_ref=send.at[peer],
+                    dst_ref=recv.at[peer],
+                    send_sem=send_sem.at[peer],
+                    recv_sem=recv_sem.at[peer],
+                    device_id=device(peer * 2 + core),
+                    device_id_type=MESH,
+                ).wait_recv()
+                total += recv[peer]
+            return total
 
         def finish():
-            def wait(step, carry):
-                copy_to(peer_at(step)).wait_send()
-                return carry
-
-            lax.fori_loop(1, n, wait, 0)
-
-        return total, finish
-
-    sums, finish1 = exchange(send1, recv1, send_sem1, recv_sem1)
-    sums = jnp.where(filt_ref[me] == 1, sums, 0.0)
+            swap.wait_send()
+            for copy in copies:
+                copy.wait_send()
+
+        return receive, finish
+
+    receive1, finish1 = exchange(local1, pair1, send1, recv1, 0, send_sem1, recv_sem1)
+    for load in loads:
+        load.wait()
+    sums = jnp.where(filt_ref[...] == 1, receive1(), 0.0)
 
     half = CATS // 2
     ids = ids_of(half)
@@ -166,10 +206,10 @@
         weight_ref[:CATS, :], attrs, preferred_element_type=jnp.float32
     ) + jnp.dot(weight_ref[CATS:, :], attrs, preferred_element_type=jnp.float32)
     for o in range(n):
-        send2[o] = totals[o * cat_rows : (o + 1) * cat_rows, :]
-    result, finish2 = exchange(send2, recv2, send_sem2, recv_sem2)
-    out_ref[...] = result
+        local2[o % 2, o // 2] = totals[o * cat_rows : (o + 1) * cat_rows, :]
+    receive2, finish2 = exchange(local2, pair2, send2, recv2, 2, send_sem2, recv_sem2)
     finish1()
+    out_ref[...] = receive2()
     finish2()
 
 
@@ -182,29 +222,33 @@
         key_hi, key_lo = filter_bits.shape
         own, width = attributes.shape
         lines = rows // LANES
-        sums_shape = (n, key_hi // n, key_lo)
-        part_shape = (n, CATS // n, width)
+        chips = n // 2
+        sums_shape = (chips, key_hi // n, key_lo)
+        part_shape = (chips, CATS // n, width)
         vmem = pl.BlockSpec(memory_space=pltpu.VMEM)
+        hbm = pl.BlockSpec(memory_space=pl.ANY)
+        exchanged = []
+        for shape in (sums_shape, part_shape):
+            exchanged.append(pltpu.VMEM((2,) + shape, jnp.float32))
+            exchanged += [pltpu.VMEM(shape, jnp.float32)] * 3
         return pl.pallas_call(
             functools.partial(kernel, n_fact, n_dim),
             out_shape=jax.ShapeDtypeStruct((CATS // n, width), jnp.float32),
-            in_specs=[vmem] * 5,
+            in_specs=[vmem, vmem, hbm, hbm, hbm],
             out_specs=vmem,
             scratch_shapes=[
                 pltpu.VMEM((lines, LANES), jnp.float32),
                 pltpu.VMEM((lines, LANES), jnp.float32),
                 pltpu.VMEM((lines, LANES), jnp.float32),
                 pltpu.VMEM((key_hi, key_lo), jnp.float32),
-                pltpu.VMEM(sums_shape, jnp.float32),
-                pltpu.VMEM(sums_shape, jnp.float32),
+                pltpu.VMEM((key_hi // n, key_lo), jnp.int32),
+                pltpu.VMEM((own // LANES, LANES), jnp.int32),
+                pltpu.VMEM((own, width), jnp.bfloat16),
                 pltpu.VMEM((2 * CATS, own), jnp.bfloat16),
-                pltpu.VMEM(part_shape, jnp.float32),
-                pltpu.VMEM(part_shape, jnp.float32),
-                pltpu.SemaphoreType.DMA((n,)),
-                pltpu.SemaphoreType.DMA((n,)),
-                pltpu.SemaphoreType.DMA((n,)),
-                pltpu.SemaphoreType.DMA((n,)),
-            ],
+            ]
+            + exchanged
+            + [pltpu.SemaphoreType.DMA((3,)), pltpu.SemaphoreType.DMA((4,))]
+            + [pltpu.SemaphoreType.DMA((chips,))] * 4,
             compiler_params=pltpu.CompilerParams(collective_id=0, has_side_effects=True),
         )(
             fact_keys.reshape(lines, LANES),

time: 34.7 us -> 33 us (0.951)
  the two profiles are of different devices: /device:TPU:25 before, /device:TPU:0 now
where the time goes in v2:
time: 33 us; the launch traced here: 32.8 us
  Pallas kernels  31.5 us (95%)
  local copies, waits for them, and re-layouts  1.3 us (4%)
    pallas_call x1, Pallas kernels, per_device(): pl.pallas_call(functools.partial(kernel, n_fact, n_dim), out_shape=jax.Sh...  31.5 us
    unnamed x1, local copies, waits for them, and re-layouts  1.3 us

profile of v2, /device:TPU:0, one launch (start us, length us, event | category | flops | bytes accessed | tf_op | source)
XLA Modules:
  0.0 32.8 jit_solution(4124573114997882630)
XLA Ops:
  0.0 31.5 %shard_map.55 = f32[16,128]{1,0:T(8,128)} custom-call(s32[256,128]{1,0:T(8,128)} %bitcast.5, bf16[256,128]{1,0:T(8,128)(2,1)} %bitcast.6, s32[32,8,256]{2,1,0:T(8,128)} %bitcast.4, s32[16,128]{1,0:T(8,128)} %bitcast.7, bf16[2048,128]{1,0:T(8,128)(2,1)} %attr_hbm.1), custom_call_target="tpu_custom_call" | custom-call | tf_op jit(solution)/shard_map/pallas_call | solution.py:234
  31.5 1.3 %copy.7 = f32[16,128]{1,0:T(8,128)} copy(f32[16,128]{1,0:T(8,128)} %shard_map.55) | data formatting | bytes 16384

commit v3 on v2

--- a/solution.py
+++ b/solution.py
@@ -1,4 +1,5 @@
 import functools
+import math
 
 import jax
 import jax.numpy as jnp
@@ -24,12 +25,14 @@
 def kernel(
     n_fact,
     n_dim,
-    keys_ref,
-    rev_ref,
+    keys_hbm,
+    rev_hbm,
     filt_hbm,
     cat_hbm,
     attr_hbm,
     out_ref,
+    keys_ref,
+    rev_ref,
     high_ref,
     low_ref,
     value_ref,
@@ -37,6 +40,7 @@
     filt_ref,
     cat_ref,
     attr_ref,
+    hot_ref,
     weight_ref,
     local1,
     pair1,
@@ -83,18 +87,25 @@
     targets = [chip_at(step) for step in range(1, chips)][::-1]
     sources = [source_at(step) for step in range(1, chips)]
 
+    first_loads = [
+        pltpu.make_async_copy(keys_hbm, keys_ref, load_sem.at[3]),
+        pltpu.make_async_copy(rev_hbm, rev_ref, load_sem.at[4]),
+    ]
+    for load in first_loads:
+        load.start()
     loads = [
         pltpu.make_async_copy(attr_hbm, attr_ref, load_sem.at[0]),
         pltpu.make_async_copy(filt_hbm.at[me], filt_ref, load_sem.at[1]),
         pltpu.make_async_copy(cat_hbm, cat_ref, load_sem.at[2]),
     ]
-    for load in loads:
-        load.start()
-
     barrier = pltpu.get_barrier_semaphore()
     for peer in [partner] + [t * 2 + core for t in targets]:
         pl.semaphore_signal(barrier, inc=1, device_id=device(peer), device_id_type=MESH)
 
+    for load in loads:
+        load.start()
+    for load in first_loads:
+        load.wait()
     keys = keys_ref[...]
     high_ref[...] = (keys // key_lo).astype(jnp.float32)
     low_ref[...] = lax.rem(keys, key_lo).astype(jnp.float32)
@@ -102,7 +113,7 @@
     acc_ref[...] = jnp.zeros_like(acc_ref)
 
     lines = keys_ref.shape[0]
-    step_lines = 8
+    step_lines = math.gcd(lines, 64)
     one = jnp.ones((), jnp.bfloat16)
     zero = jnp.zeros((), jnp.bfloat16)
 
@@ -182,29 +193,32 @@
     receive1, finish1 = exchange(local1, pair1, send1, recv1, 0, send_sem1, recv_sem1)
     for load in loads:
         load.wait()
-    sums = jnp.where(filt_ref[...] == 1, receive1(), 0.0)
 
     half = CATS // 2
     ids = ids_of(half)
     per_row = key_lo // LANES
-    for j in range(own_rows * per_row):
-        r, c = j // per_row, j % per_row
-        own = sums[r : r + 1, c * LANES : (c + 1) * LANES]
+    chunks = own_rows * per_row
+    for j in range(chunks):
         cat = cat_ref[j : j + 1, :]
-        upper = cat >= half
-        match = rows_of(jnp.where(upper, cat - half, cat).astype(jnp.float32), half) == ids
-        first = own.astype(jnp.bfloat16).astype(jnp.float32)
-        for t, term in enumerate((first, own - first)):
-            for h in range(2):
-                part = jnp.where(upper == (h == 1), term, 0.0)
-                base = t * CATS + h * half
-                weight_ref[base : base + half, j * LANES : (j + 1) * LANES] = jnp.where(
-                    match, rows_of(part, half), zero
-                )
-    attrs = attr_ref[...]
-    totals = jnp.dot(
-        weight_ref[:CATS, :], attrs, preferred_element_type=jnp.float32
-    ) + jnp.dot(weight_ref[CATS:, :], attrs, preferred_element_type=jnp.float32)
+        for h, local in enumerate((jnp.where(cat < half, cat, -1), cat - half)):
+            hot_ref[h * half : (h + 1) * half, j * LANES : (j + 1) * LANES] = jnp.where(
+                rows_of(local.astype(jnp.float32), half) == ids, one, zero
+            )
+
+    sums = jnp.where(filt_ref[...] == 1, receive1(), 0.0)
+    stacked = [sums[:, c * LANES : (c + 1) * LANES] for c in range(per_row)]
+    stacked.append(jnp.zeros((LANES - chunks, LANES), jnp.float32))
+    columns = jnp.concatenate(stacked, axis=0).T
+    width = attr_ref.shape[1]
+    for j in range(chunks):
+        i = j % per_row * own_rows + j // per_row
+        keys_at = slice(j * LANES, (j + 1) * LANES)
+        product = columns[:, i : i + 1] * attr_ref[keys_at, :].astype(jnp.float32)
+        first = product.astype(jnp.bfloat16)
+        weight_ref[keys_at, :width] = first
+        weight_ref[keys_at, width:] = (product - first.astype(jnp.float32)).astype(jnp.bfloat16)
+    both = jnp.dot(hot_ref[...], weight_ref[...], preferred_element_type=jnp.float32)
+    totals = both[:, :width] + both[:, width:]
     for o in range(n):
         local2[o % 2, o // 2] = totals[o * cat_rows : (o + 1) * cat_rows, :]
     receive2, finish2 = exchange(local2, pair2, send2, recv2, 2, send_sem2, recv_sem2)
@@ -234,9 +248,11 @@
         return pl.pallas_call(
             functools.partial(kernel, n_fact, n_dim),
             out_shape=jax.ShapeDtypeStruct((CATS // n, width), jnp.float32),
-            in_specs=[vmem, vmem, hbm, hbm, hbm],
+            in_specs=[hbm] * 5,
             out_specs=vmem,
             scratch_shapes=[
+                pltpu.VMEM((lines, LANES), jnp.int32),
+                pltpu.VMEM((lines, LANES), jnp.bfloat16),
                 pltpu.VMEM((lines, LANES), jnp.float32),
                 pltpu.VMEM((lines, LANES), jnp.float32),
                 pltpu.VMEM((lines, LANES), jnp.float32),
@@ -244,10 +260,11 @@
                 pltpu.VMEM((key_hi // n, key_lo), jnp.int32),
                 pltpu.VMEM((own // LANES, LANES), jnp.int32),
                 pltpu.VMEM((own, width), jnp.bfloat16),
-                pltpu.VMEM((2 * CATS, own), jnp.bfloat16),
+                pltpu.VMEM((CATS, own), jnp.bfloat16),
+                pltpu.VMEM((own, 2 * width), jnp.bfloat16),
             ]
             + exchanged
-            + [pltpu.SemaphoreType.DMA((3,)), pltpu.SemaphoreType.DMA((4,))]
+            + [pltpu.SemaphoreType.DMA((5,)), pltpu.SemaphoreType.DMA((4,))]
             + [pltpu.SemaphoreType.DMA((chips,))] * 4,
             compiler_params=pltpu.CompilerParams(collective_id=0, has_side_effects=True),
         )(

time: 33 us -> 26.7 us (0.81)
  Pallas kernels: 31.5 us -> 25.2 us
    pallas_call x1, Pallas kernels: 31.5 us -> 25.2 us  [per_device(): pl.pallas_call(functools.partial(kernel, n_fact, n_dim), out_shape=jax.Sh...]
where the time goes in v3:
time: 26.7 us; the launch traced here: 26.5 us
  Pallas kernels  25.2 us (94%)
  local copies, waits for them, and re-layouts  1.3 us (5%)
    pallas_call x1, Pallas kernels, per_device(): pl.pallas_call(functools.partial(kernel, n_fact, n_dim), out_shape=jax.Sh...  25.2 us
    unnamed x1, local copies, waits for them, and re-layouts  1.3 us

profile of v3, /device:TPU:0, one launch (start us, length us, event | category | flops | bytes accessed | tf_op | source)
XLA Modules:
  0.0 26.5 jit_solution(2504110816808350363)
XLA Ops:
  0.0 25.2 %shard_map.55 = f32[16,128]{1,0:T(8,128)} custom-call(s32[256,128]{1,0:T(8,128)} %bitcast.5, bf16[256,128]{1,0:T(8,128)(2,1)} %bitcast.6, s32[32,8,256]{2,1,0:T(8,128)} %bitcast.4, s32[16,128]{1,0:T(8,128)} %bitcast.7, bf16[2048,128]{1,0:T(8,128)(2,1)} %attr_hbm.1), custom_call_target="tpu_custom_call" | custom-call | tf_op jit(solution)/shard_map/pallas_call | solution.py:248
  25.2 1.3 %copy.7 = f32[16,128]{1,0:T(8,128)} copy(f32[16,128]{1,0:T(8,128)} %shard_map.55) | data formatting | bytes 16384

commit v4 on v3

--- a/solution.py
+++ b/solution.py
@@ -20,6 +20,18 @@
 
 def ids_of(count):
     return lax.broadcasted_iota(jnp.int32, (count, LANES), 0).astype(jnp.float32).astype(jnp.bfloat16)
+
+
+def encode(sums, middle, rate):
+    blocks = [sums[:, c : c + LANES] for c in range(0, sums.shape[1], LANES)]
+    stacked = jnp.concatenate(blocks, axis=0)
+    code = jnp.floor((jnp.log2(stacked) - middle) * rate + 0.5)
+    return jnp.where(stacked > 0, code, -32768.0).astype(jnp.int32).astype(jnp.int16)
+
+
+def decode(codes, middle, rate):
+    wide = codes.astype(jnp.int32)
+    return jnp.where(wide > -32768, jnp.exp2(wide.astype(jnp.float32) * (1 / rate) + middle), 0.0)
 
 
 def kernel(
@@ -44,6 +56,7 @@
     weight_ref,
     local1,
     pair1,
+    whole1,
     send1,
     recv1,
     local2,
@@ -113,7 +126,7 @@
     acc_ref[...] = jnp.zeros_like(acc_ref)
 
     lines = keys_ref.shape[0]
-    step_lines = math.gcd(lines, 64)
+    step_lines = math.gcd(lines, 128)
     one = jnp.ones((), jnp.bfloat16)
     zero = jnp.zeros((), jnp.bfloat16)
 
@@ -143,7 +156,10 @@
 
     pl.semaphore_wait(barrier, chips)
 
-    def exchange(local, pair, send, recv, sems, send_sem, recv_sem):
+    least, most = -3.5, math.log2(2 * lines * LANES) + 0.5
+    middle, rate = (least + most) / 2, 65000 / (most - least)
+
+    def exchange(local, pair, send, recv, sems, send_sem, recv_sem, whole=None):
         swap = pltpu.make_async_remote_copy(
             src_ref=local.at[1 - core],
             dst_ref=pair,
@@ -154,7 +170,12 @@
         )
         swap.start()
         swap.wait_recv()
-        send[...] = local[core] + pair[...]
+        if whole is None:
+            send[...] = local[core] + pair[...]
+        else:
+            whole[...] = local[core] + pair[...]
+            for i in range(chips):
+                send[i] = encode(whole[i], middle, rate)
         copies = [
             pltpu.make_async_remote_copy(
                 src_ref=send.at[peer],
@@ -170,7 +191,12 @@
             copy.start()
 
         def receive():
-            total = send[chip]
+            if whole is None:
+                total = send[chip]
+            else:
+                own = whole[chip]
+                blocks = [own[:, c : c + LANES] for c in range(0, own.shape[1], LANES)]
+                total = jnp.concatenate(blocks, axis=0)
             for peer in sources:
                 pltpu.make_async_remote_copy(
                     src_ref=send.at[peer],
@@ -180,7 +206,7 @@
                     device_id=device(peer * 2 + core),
                     device_id_type=MESH,
                 ).wait_recv()
-                total += recv[peer]
+                total += recv[peer] if whole is None else decode(recv[peer], middle, rate)
             return total
 
         def finish():
@@ -190,7 +216,7 @@
 
         return receive, finish
 
-    receive1, finish1 = exchange(local1, pair1, send1, recv1, 0, send_sem1, recv_sem1)
+    receive1, finish1 = exchange(local1, pair1, send1, recv1, 0, send_sem1, recv_sem1, whole1)
     for load in loads:
         load.wait()
 
@@ -205,9 +231,9 @@
                 rows_of(local.astype(jnp.float32), half) == ids, one, zero
             )
 
-    sums = jnp.where(filt_ref[...] == 1, receive1(), 0.0)
-    stacked = [sums[:, c * LANES : (c + 1) * LANES] for c in range(per_row)]
-    stacked.append(jnp.zeros((LANES - chunks, LANES), jnp.float32))
+    filt = [filt_ref[:, c * LANES : (c + 1) * LANES] for c in range(per_row)]
+    sums = jnp.where(jnp.concatenate(filt, axis=0) == 1, receive1(), 0.0)
+    stacked = [sums, jnp.zeros((LANES - chunks, LANES), jnp.float32)]
     columns = jnp.concatenate(stacked, axis=0).T
     width = attr_ref.shape[1]
     for j in range(chunks):
@@ -241,10 +267,11 @@
         part_shape = (chips, CATS // n, width)
         vmem = pl.BlockSpec(memory_space=pltpu.VMEM)
         hbm = pl.BlockSpec(memory_space=pl.ANY)
-        exchanged = []
-        for shape in (sums_shape, part_shape):
-            exchanged.append(pltpu.VMEM((2,) + shape, jnp.float32))
-            exchanged += [pltpu.VMEM(shape, jnp.float32)] * 3
+        codes = pltpu.VMEM((chips, own // LANES, LANES), jnp.int16)
+        exchanged = [pltpu.VMEM((2,) + sums_shape, jnp.float32)]
+        exchanged += [pltpu.VMEM(sums_shape, jnp.float32)] * 2 + [codes] * 2
+        exchanged += [pltpu.VMEM((2,) + part_shape, jnp.float32)]
+        exchanged += [pltpu.VMEM(part_shape, jnp.float32)] * 3
         return pl.pallas_call(
             functools.partial(kernel, n_fact, n_dim),
             out_shape=jax.ShapeDtypeStruct((CATS // n, width), jnp.float32),

time: 26.7 us -> 25.2 us (0.944)
  Pallas kernels: 25.2 us -> 23.7 us
    pallas_call x1, Pallas kernels: 25.2 us -> 23.7 us  [per_device(): pl.pallas_call(functools.partial(kernel, n_fact, n_dim), out_shape=jax.Sh...]
where the time goes in v4:
time: 25.2 us; the launch traced here: 25 us
  Pallas kernels  23.7 us (94%)
  local copies, waits for them, and re-layouts  1.3 us (5%)
    pallas_call x1, Pallas kernels, per_device(): pl.pallas_call(functools.partial(kernel, n_fact, n_dim), out_shape=jax.Sh...  23.7 us
    unnamed x1, local copies, waits for them, and re-layouts  1.3 us

profile of v4, /device:TPU:0, one launch (start us, length us, event | category | flops | bytes accessed | tf_op | source)
XLA Modules:
  0.0 25.0 jit_solution(10796335985552570355)
XLA Ops:
  0.0 23.7 %shard_map.55 = f32[16,128]{1,0:T(8,128)} custom-call(s32[256,128]{1,0:T(8,128)} %bitcast.5, bf16[256,128]{1,0:T(8,128)(2,1)} %bitcast.6, s32[32,8,256]{2,1,0:T(8,128)} %bitcast.4, s32[16,128]{1,0:T(8,128)} %bitcast.7, bf16[2048,128]{1,0:T(8,128)(2,1)} %attr_hbm.1), custom_call_target="tpu_custom_call" | custom-call | tf_op jit(solution)/shard_map/pallas_call | solution.py:275
  23.7 1.3 %copy.7 = f32[16,128]{1,0:T(8,128)} copy(f32[16,128]{1,0:T(8,128)} %shard_map.55) | data formatting | bytes 16384
